TPU v7x, 32 devices: a whole 2x2x4 slice. The times are simulated.
32 devices in a mesh: tile: 8 (over y, x, core), bulk: 4 (over z).
Axes of the slice: x: 2, y: 2, z: 4, core: 2. Of those that a mesh axis runs over, the one named last changes fastest.
Arguments:
- integrals: bfloat16 [96, 256, 768], P(('tile', 'bulk')), may hold values from -0.21875 to 0.21875
- amplitudes: bfloat16 [4, 768, 1024], P(None, 'bulk', 'tile'), may hold values from -6 to 6
- residual_in: bfloat16 [96, 256, 1024], P(('tile', 'bulk')), may hold values from -6 to 6
- tile_irrep: int32 [96], replicated, may hold values from 0 to 3, as said below
Outputs:
- residual: bfloat16 [96, 256, 1024], P(('tile', 'bulk'))
Inputs may be any that keep to these rules, and one draw needn't show every extreme that they name: tile_irrep never falls along the tiles, and every irrep labels at least 12 tiles.
All inputs are finite; a program needn't handle non-finite values.
Results may differ from a plain program's by a relative error of at most 0.001.
Values may be sent and summed in bfloat16 or wider, within the bound.
A program may use at most 64 MiB of HBM per device.

v0:
```python
import functools

import jax
import jax.numpy as jnp
from jax import lax
from jax.experimental import pallas as pl
from jax.experimental.pallas import tpu as pltpu
from jax.sharding import PartitionSpec as P

MESH = pl.DeviceIdType.MESH
PARTS = 2


def gathered_plan(integrals, amplitudes, residual_in, tile_irrep):
    tile_dev = integrals.shape[0]
    first_tile = (lax.axis_index("tile") * lax.axis_size("bulk") + lax.axis_index("bulk")) * tile_dev
    local_irrep = lax.dynamic_slice_in_dim(tile_irrep, first_tile, tile_dev, 0)
    whole_cd = lax.all_gather(amplitudes, "bulk", axis=1, tiled=True)
    picked = jnp.take(lax.all_gather(whole_cd, "tile", axis=2, tiled=True), local_irrep, axis=0)
    product = jnp.einsum("trc,tcp->trp", integrals, picked, preferred_element_type=jnp.float32)
    return (residual_in.astype(jnp.float32) + product).astype(jnp.bfloat16)


def kernel(rows, bulk, slots, parts, irrep_ref, amp_hbm, int_hbm, res_hbm, out_ref, *scratch):
    cols = rows // 2
    offsets = [0] + [s * d for d in range(1, bulk) for s in (-1, 1)]
    chunks = len(offsets)
    (amp, ints, res, whole), scratch = scratch[:4], scratch[4:]
    held = [[None] * parts] + [list(scratch[i * parts:(i + 1) * parts]) for i in range(chunks - 1)]
    scratch = scratch[(chunks - 1) * parts:]
    picked = [list(scratch[i * parts:(i + 1) * parts]) for i in range(chunks)]
    (z_send, z_recv, c_send, c_recv, p_send, p_recv, local_sem) = scratch[chunks * parts:]
    tiles = ints.shape[0]
    irreps, depth, width = amp.shape
    piece = depth // parts
    me, at = lax.axis_index("tile"), lax.axis_index("bulk")
    col, core = me // 2, me % 2
    partner = col * 2 + (1 - core)

    amp_copy = pltpu.make_async_copy(amp_hbm, amp, local_sem.at[0])
    int_copy = pltpu.make_async_copy(int_hbm, ints, local_sem.at[1])
    res_copy = pltpu.make_async_copy(res_hbm, res, local_sem.at[2])
    amp_copy.start()

    barrier = pltpu.get_barrier_semaphore()
    pl.semaphore_signal(barrier, inc=1, device_id=(partner, at), device_id_type=MESH)
    for j in range(1, cols):
        pl.semaphore_signal(barrier, inc=1, device_id=(lax.rem(col + j, cols) * 2 + core, at), device_id_type=MESH)

    @pl.when(at > 0)
    def _():
        pl.semaphore_signal(barrier, inc=1, device_id=(me, at - 1), device_id_type=MESH)

    @pl.when(at < bulk - 1)
    def _():
        pl.semaphore_signal(barrier, inc=1, device_id=(me, at + 1), device_id_type=MESH)

    int_copy.start()
    res_copy.start()
    pl.semaphore_wait(barrier, cols + (at > 0).astype(jnp.int32) + (at < bulk - 1).astype(jnp.int32))

    amp_copy.wait()

    def block(c, p):
        if c == 0:
            return amp.at[:, pl.ds(p * piece, piece), :]
        return held[c][p]

    def line(c, p, step):
        there = offsets.index(offsets[c] - step)
        way = 0 if step > 0 else 1
        return pltpu.make_async_remote_copy(
            src_ref=block(c, p), dst_ref=held[there][p], send_sem=z_send.at[way, c, p],
            recv_sem=z_recv.at[there, p], device_id=(me, at + step), device_id_type=MESH)

    def line_in(c, p):
        return pltpu.make_async_remote_copy(
            src_ref=held[c][p], dst_ref=held[c][p], send_sem=z_send.at[0, c, p],
            recv_sem=z_recv.at[c, p], device_id=(partner, at), device_id_type=MESH)

    def slab(c, p, row):
        first = pl.multiple_of((at + offsets[c]) * depth + p * piece, 16)
        return whole.at[:, pl.ds(first, piece), pl.ds(pl.multiple_of(row * width, 128), width)]

    def across(c, p, j):
        return pltpu.make_async_remote_copy(
            src_ref=picked[c][p].at[j - 1], dst_ref=slab(c, p, me), send_sem=c_send.at[c, p, j],
            recv_sem=c_recv.at[c, p, j], device_id=(lax.rem(col + j, cols) * 2 + core, at), device_id_type=MESH)

    def over(c, p, j, side):
        row = lax.rem(col - j + cols, cols) * 2 + side
        return pltpu.make_async_remote_copy(
            src_ref=slab(c, p, row), dst_ref=slab(c, p, row), send_sem=p_send.at[c, p, j],
            recv_sem=p_recv.at[c, p, j], device_id=(partner, at), device_id_type=MESH)

    def wanted(column):
        low = (2 * column * bulk + at) * tiles
        high = ((2 * column + 1) * bulk + at) * tiles + tiles - 1
        spots = [low, high] if slots == 2 else [low, low + tiles - 1, high]
        return [irrep_ref[s] for s in spots]

    def present(c):
        src = at + offsets[c]
        return jnp.logical_and(src >= 0, src < bulk)

    def relay(c, p):
        if offsets[c] <= 0:
            @pl.when(at < bulk - 1)
            def _():
                line(c, p, 1).start()
        if offsets[c] >= 0:
            @pl.when(at > 0)
            def _():
                line(c, p, -1).start()

    def relay_done(c, p):
        if offsets[c] <= 0 and offsets[c] - 1 > -bulk:
            @pl.when(at < bulk - 1)
            def _():
                line(c, p, 1).wait_send()
        if offsets[c] >= 0 and offsets[c] + 1 < bulk:
            @pl.when(at > 0)
            def _():
                line(c, p, -1).wait_send()

    def spread(c, p):
        src = amp if c == 0 else held[c][p]
        lanes = pl.ds(p * piece, piece) if c == 0 else slice(None)
        for j in range(1, cols):
            for s, g in enumerate(wanted(lax.rem(col + j, cols))):
                picked[c][p][j - 1, s] = src[g, lanes, :]
            across(c, p, j).start()
        first = pl.multiple_of((at + offsets[c]) * depth + p * piece, 16)
        for s, g in enumerate(wanted(col)):
            whole[s, pl.ds(first, piece), pl.ds(pl.multiple_of(me * width, 128), width)] = src[g, lanes, :]
        over(c, p, 0, core).start()

    def forward(c, p):
        for j in range(1, cols):
            across_in = pltpu.make_async_remote_copy(
                src_ref=slab(c, p, lax.rem(col - j + cols, cols) * 2 + core),
                dst_ref=slab(c, p, lax.rem(col - j + cols, cols) * 2 + core),
                send_sem=c_send.at[c, p, j], recv_sem=c_recv.at[c, p, j],
                device_id=(partner, at), device_id_type=MESH)
            across_in.wait_recv()
            over(c, p, j, core).start()

    for p in range(parts):
        relay(0, p)
    for p in range(parts):
        spread(0, p)
    groups = [[(0, p) for p in range(parts)]]
    for d in range(1, bulk):
        groups.append([(c, p) for p in range(parts) for c in (2 * d - 1, 2 * d)])
    for d in range(1, bulk):
        for c, p in groups[d]:
            @pl.when(present(c))
            def _():
                line_in(c, p).wait_recv()
                if abs(offsets[c]) < bulk - 1:
                    relay(c, p)
                spread(c, p)
        for c, p in groups[d - 1]:
            @pl.when(present(c))
            def _():
                forward(c, p)
    for c, p in groups[bulk - 1]:
        @pl.when(present(c))
        def _():
            forward(c, p)
    int_copy.wait()
    res_copy.wait()
    for group in groups:
        for c, p in group:
            @pl.when(present(c))
            def _():
                for j in range(cols):
                    over(c, p, j, 1 - core).wait_recv()

    mine = wanted(col)
    first_tile = (me * bulk + at) * tiles
    columns = whole.shape[2]
    block_n = 512 if columns % 512 == 0 else 128

    for t in range(tiles):
        irrep = irrep_ref[first_tile + t]
        slot = (irrep > mine[0]).astype(jnp.int32)
        for s in mine[1:-1]:
            slot = slot + (irrep > s).astype(jnp.int32)

        @pl.loop(0, columns // block_n)
        def _(n):
            span = pl.ds(pl.multiple_of(n * block_n, block_n), block_n)
            ladder = jnp.dot(ints[t], whole[slot, :, span], preferred_element_type=jnp.float32)
            out_ref[t, :, span] = (res[t, :, span].astype(jnp.float32) + ladder).astype(jnp.bfloat16)

    for group in groups:
        for c, p in group:
            @pl.when(present(c))
            def _():
                for j in range(cols):
                    over(c, p, j, core).wait_send()
                for j in range(1, cols):
                    across(c, p, j).wait_send()
                relay_done(c, p)

def call(rows, bulk, slots, integrals, amplitudes, residual_in, tile_irrep):
    irreps, depth, width = amplitudes.shape
    parts = PARTS if depth % (16 * PARTS) == 0 else 1
    chunks = 2 * bulk - 1
    cols = rows // 2
    any_space = pl.BlockSpec(memory_space=pl.ANY)
    return pl.pallas_call(
        functools.partial(kernel, rows, bulk, slots, parts),
        out_shape=jax.ShapeDtypeStruct(residual_in.shape, residual_in.dtype),
        in_specs=[pl.BlockSpec(memory_space=pltpu.SMEM), any_space, any_space, any_space],
        out_specs=pl.BlockSpec(memory_space=pltpu.VMEM),
        scratch_shapes=[
            pltpu.VMEM(amplitudes.shape, amplitudes.dtype),
            pltpu.VMEM(integrals.shape, integrals.dtype),
            pltpu.VMEM(residual_in.shape, residual_in.dtype),
            pltpu.VMEM((slots, depth * bulk, width * rows), amplitudes.dtype),
            *[pltpu.VMEM((irreps, depth // parts, width), amplitudes.dtype)] * ((chunks - 1) * parts),
            *[pltpu.VMEM((cols - 1, slots, depth // parts, width), amplitudes.dtype)] * (chunks * parts),
            pltpu.SemaphoreType.DMA((2, chunks, parts)),
            pltpu.SemaphoreType.DMA((chunks, parts)),
            pltpu.SemaphoreType.DMA((chunks, parts, cols)),
            pltpu.SemaphoreType.DMA((chunks, parts, cols)),
            pltpu.SemaphoreType.DMA((chunks, parts, cols)),
            pltpu.SemaphoreType.DMA((chunks, parts, cols)),
            pltpu.SemaphoreType.DMA((3,)),
        ],
        compiler_params=pltpu.CompilerParams(collective_id=slots, has_side_effects=True),
    )(tile_irrep, amplitudes, integrals, residual_in)


def local(rows, bulk, integrals, amplitudes, residual_in, tile_irrep):
    depth, width = amplitudes.shape[1:]
    if rows % 2 or rows < 4 or bulk < 2 or depth % 16 or width % 128:
        return gathered_plan(integrals, amplitudes, residual_in, tile_irrep)
    ends = tile_irrep.reshape(rows // 2, 2, bulk, integrals.shape[0])
    low, high = ends[:, 0, :, 0], ends[:, 1, :, -1]
    mid = ends[:, 0, :, -1]
    mid_too = ends[:, 1, :, 0]
    third = jnp.any(((mid != low) & (mid != high)) | ((mid_too != low) & (mid_too != high)))
    return lax.cond(
        third,
        functools.partial(call, rows, bulk, 3),
        functools.partial(call, rows, bulk, 2),
        integrals, amplitudes, residual_in, tile_irrep)


def solution(mesh):
    return jax.shard_map(
        functools.partial(local, mesh.shape["tile"], mesh.shape["bulk"]),
        mesh=mesh,
        in_specs=(
            P(("tile", "bulk"), None, None),
            P(None, "bulk", "tile"),
            P(("tile", "bulk"), None, None),
            P(),
        ),
        out_specs=P(("tile", "bulk"), None, None),
        check_vma=False,
    )
```

profile of v0, /device:TPU:1, one launch (start us, length us, event | category | flops | bytes accessed | tf_op | source)
XLA Modules:
  0.0 32.4 jit_solution(9227728659625788692)
XLA Ops:
  0.0 0.8 %reshape.10 = s32[4,2,4,3]{3,2,1,0:T(4,128)S(1)} reshape(s32[96]{0:T(128)} %param.9) | data formatting | bytes 768 | tf_op jit(solution)/shard_map/reshape | solution.py:241
  0.8 0.7 %or_reduce_fusion = pred[]{:T(512)} fusion(s32[4,2,4,3]{3,2,1,0:T(4,128)S(1)} %reshape.10), kind=kLoop, calls=%fused_computation | loop fusion | flops 127 | bytes 257 | tf_op jit(solution)/shard_map/reduce_or | solution.py:245
  2.1 29.2 %conditional.1 = (bf16[3,256,1024]{2,1,0:T(8,128)(2,1)S(1)}) conditional(s32[]{:T(128)} %convert_element_type.3, (s32[96]{0:T(128)}, bf16[4,192,128]{2,1,0:T(8,128)(2,1)}, bf16[3,256,768]{2,1,0:T(8,128)(2,1)}, bf16[3,256,1024]{2,1,0:T(8,128)(2,1)}) %tuple.11, (s32[96]{0:T(128)}, bf16[4,192,128]{2,1,0:T(8,128)(2,1)}, bf16[3,256,768]{2,1,0:T(8,128)(2,1)}, ...), branch_computations={%region_1.0_spmd, %region_2.0_spmd} | conditional | bytes 8 | solution.py:246
  2.2 29.1 %branch_0_fun.1 = bf16[3,256,1024]{2,1,0:T(8,128)(2,1)S(1)} custom-call(s32[96]{0:T(128)} %get-tuple-element.24.irrep_ref, bf16[4,192,128]{2,1,0:T(8,128)(2,1)} %get-tuple-element.39.amp_hbm, bf16[3,256,768]{2,1,0:T(8,128)(2,1)} %get-tuple-element.41.int_hbm, bf16[3,256,1024]{2,1,0:T(8,128)(2,1)} %get-tuple-element.43.res_hbm), custom_call_target="tpu_custom_call" | custom-call | tf_op jit(solution)/shard_map/cond/branch_0_fun/pallas_call | solution.py:213
  31.3 1.1 %copy.16 = bf16[3,256,1024]{2,1,0:T(8,128)(2,1)} copy(bf16[3,256,1024]{2,1,0:T(8,128)(2,1)S(1)} %get-tuple-element.32) | data formatting | bytes 3145728
where the time goes:
time: 32.6 us; the launch traced here: 32.4 us
  Pallas kernels  29.1 us (89%)
  local copies, waits for them, and re-layouts  1.91 us (6%)
  other arithmetic  0.73 us (2%)
  between operations  0.67 us (2%)
    pallas_call x1, Pallas kernels, call(): pl.pallas_call(functools.partial(kernel, rows, bulk, slots, parts), out_s...  29.1 us
    unnamed x1, local copies, waits for them, and re-layouts  1.15 us
    reshape x1, local copies, waits for them, and re-layouts, local(): ends = tile_irrep.reshape(rows // 2, 2, bulk, integrals.shape[0])  0.76 us
    reduce_or x1, other arithmetic, local(): jnp.any((mid != low) & (mid != high) | (mid_too != low) & (mid_too != high))  0.73 us

commit v1 on v0

v1 whole, which is shorter than its diff:
```python
import functools

import jax
import jax.numpy as jnp
from jax import lax
from jax.experimental import pallas as pl
from jax.experimental.pallas import tpu as pltpu
from jax.sharding import PartitionSpec as P

MESH = pl.DeviceIdType.MESH
PARTS = 2
VMEM_LIMIT = 32 << 20


def gathered_plan(integrals, amplitudes, residual_in, tile_irrep):
    tile_dev = integrals.shape[0]
    first_tile = (lax.axis_index("tile") * lax.axis_size("bulk") + lax.axis_index("bulk")) * tile_dev
    local_irrep = lax.dynamic_slice_in_dim(tile_irrep, first_tile, tile_dev, 0)
    whole_cd = lax.all_gather(amplitudes, "bulk", axis=1, tiled=True)
    picked = jnp.take(lax.all_gather(whole_cd, "tile", axis=2, tiled=True), local_irrep, axis=0)
    product = jnp.einsum("trc,tcp->trp", integrals, picked, preferred_element_type=jnp.float32)
    return (residual_in.astype(jnp.float32) + product).astype(jnp.bfloat16)


def kernel(rows, bulk, slots, parts, irrep_hbm, amp_hbm, int_hbm, res_hbm, out_ref, flag_ref, *scratch):
    cols = rows // 2
    offsets = [0] + [s * d for d in range(1, bulk) for s in (-1, 1)]
    chunks = len(offsets)
    (irrep_ref, amp, ints, res, lhs, total), scratch = scratch[:6], scratch[6:]
    gathered, scratch = [scratch[:chunks], scratch[chunks:2 * chunks]], scratch[2 * chunks:]
    held = [[None] * parts] + [list(scratch[i * parts:(i + 1) * parts]) for i in range(chunks - 1)]
    scratch = scratch[(chunks - 1) * parts:]
    picked = [list(scratch[i * parts:(i + 1) * parts]) for i in range(chunks)]
    (z_send, z_recv, c_send, c_recv, p_send, p_recv, local_sem) = scratch[chunks * parts:]
    tiles = ints.shape[0]
    irreps, depth, width = amp.shape
    piece = depth // parts
    me, at = lax.axis_index("tile"), lax.axis_index("bulk")
    col, core = me // 2, me % 2
    partner = col * 2 + (1 - core)

    irrep_copy = pltpu.make_async_copy(irrep_hbm, irrep_ref, local_sem.at[3])
    amp_copy = pltpu.make_async_copy(amp_hbm, amp, local_sem.at[0])
    int_copy = pltpu.make_async_copy(int_hbm, ints, local_sem.at[1])
    res_copy = pltpu.make_async_copy(res_hbm, res, local_sem.at[2])
    amp_copy.start()
    irrep_copy.start()

    barrier = pltpu.get_barrier_semaphore()
    pl.semaphore_signal(barrier, inc=1, device_id=(partner, at), device_id_type=MESH)
    for j in range(1, cols):
        pl.semaphore_signal(barrier, inc=1, device_id=(lax.rem(col + j, cols) * 2 + core, at), device_id_type=MESH)

    @pl.when(at > 0)
    def _():
        pl.semaphore_signal(barrier, inc=1, device_id=(me, at - 1), device_id_type=MESH)

    @pl.when(at < bulk - 1)
    def _():
        pl.semaphore_signal(barrier, inc=1, device_id=(me, at + 1), device_id_type=MESH)

    int_copy.start()
    res_copy.start()
    pl.semaphore_wait(barrier, cols + (at > 0).astype(jnp.int32) + (at < bulk - 1).astype(jnp.int32))

    amp_copy.wait()

    def block(c, p):
        if c == 0:
            return amp.at[:, pl.ds(p * piece, piece), :]
        return held[c][p]

    def line(c, p, step):
        there = offsets.index(offsets[c] - step)
        way = 0 if step > 0 else 1
        return pltpu.make_async_remote_copy(
            src_ref=block(c, p), dst_ref=held[there][p], send_sem=z_send.at[way, c, p],
            recv_sem=z_recv.at[there, p], device_id=(me, at + step), device_id_type=MESH)

    def line_in(c, p):
        return pltpu.make_async_remote_copy(
            src_ref=held[c][p], dst_ref=held[c][p], send_sem=z_send.at[0, c, p],
            recv_sem=z_recv.at[c, p], device_id=(partner, at), device_id_type=MESH)

    def slab(side, c, p, column):
        return gathered[side][c].at[:, pl.ds(p * piece, piece), pl.ds(pl.multiple_of(column * width, 128), width)]

    def across(c, p, j):
        return pltpu.make_async_remote_copy(
            src_ref=picked[c][p].at[j - 1], dst_ref=slab(0, c, p, col), send_sem=c_send.at[c, p, j],
            recv_sem=c_recv.at[c, p, j], device_id=(lax.rem(col + j, cols) * 2 + core, at), device_id_type=MESH)

    def over(c, p, j):
        column = lax.rem(col - j + cols, cols)
        return pltpu.make_async_remote_copy(
            src_ref=slab(0, c, p, column), dst_ref=slab(1, c, p, column), send_sem=p_send.at[c, p, j],
            recv_sem=p_recv.at[c, p, j], device_id=(partner, at), device_id_type=MESH)

    def wanted(column):
        low = (2 * column * bulk + at) * tiles
        high = ((2 * column + 1) * bulk + at) * tiles + tiles - 1
        spots = [low, high] if slots == 2 else [low, low + tiles - 1, high]
        return [irrep_ref[s] for s in spots]

    def present(c):
        src = at + offsets[c]
        return jnp.logical_and(src >= 0, src < bulk)

    def relay(c, p):
        if offsets[c] <= 0:
            @pl.when(at < bulk - 1)
            def _():
                line(c, p, 1).start()
        if offsets[c] >= 0:
            @pl.when(at > 0)
            def _():
                line(c, p, -1).start()

    def relay_done(c, p):
        if offsets[c] <= 0 and offsets[c] - 1 > -bulk:
            @pl.when(at < bulk - 1)
            def _():
                line(c, p, 1).wait_send()
        if offsets[c] >= 0 and offsets[c] + 1 < bulk:
            @pl.when(at > 0)
            def _():
                line(c, p, -1).wait_send()

    def spread(c, p):
        src = amp if c == 0 else held[c][p]
        lanes = pl.ds(p * piece, piece) if c == 0 else slice(None)
        for j in range(1, cols):
            for s, g in enumerate(wanted(lax.rem(col + j, cols))):
                picked[c][p][j - 1, s] = src[g, lanes, :]
            across(c, p, j).start()
        for s, g in enumerate(wanted(col)):
            gathered[0][c][s, pl.ds(p * piece, piece), pl.ds(pl.multiple_of(col * width, 128), width)] = src[g, lanes, :]
        over(c, p, 0).start()

    def forward(c, p):
        for j in range(1, cols):
            landed = slab(0, c, p, lax.rem(col - j + cols, cols))
            pltpu.make_async_remote_copy(
                src_ref=landed, dst_ref=landed, send_sem=c_send.at[c, p, j], recv_sem=c_recv.at[c, p, j],
                device_id=(partner, at), device_id_type=MESH).wait_recv()
            over(c, p, j).start()

    first_tile = (me * bulk + at) * tiles
    half = cols * width
    last = jnp.where(2 * at < bulk, bulk - 1, 0)

    def arrived(c):
        for p in range(parts):
            for j in range(cols):
                over(c, p, j).wait_recv()

    def product(c, side, begin, end):
        def one(t):
            irrep = irrep_ref[first_tile + t]
            slot = (irrep > mine[0]).astype(jnp.int32)
            for s in mine[1:-1]:
                slot = slot + (irrep > s).astype(jnp.int32)
            part = jnp.dot(lhs[at + offsets[c], t], gathered[side][c][slot], preferred_element_type=jnp.float32)
            if not begin:
                part = part + total[side, t]
            if not begin and not end:
                total[side, t] = part
                return
            for n in range(cols):
                there = pl.ds(pl.multiple_of((n * 2 + (core if side == 0 else 1 - core)) * width, width), width)
                here = part[:, n * width:(n + 1) * width]
                if end:
                    out_ref[t, :, there] = here.astype(jnp.bfloat16)
                else:
                    total[side, t, :, n * width:(n + 1) * width] = here + res[t, :, there].astype(jnp.float32)

        for t in range(tiles):
            one(t)

    groups = [[0]] + [[2 * d - 1, 2 * d] for d in range(1, bulk)]

    def add(d):
        for c in groups[d]:
            src = at + offsets[c]

            @pl.when(jnp.logical_and(present(c), src != last))
            def _():
                arrived(c)
                for side in range(2):
                    product(c, side, d == 0, False)

    def gather(d):
        for p in range(parts):
            for c in groups[d]:
                @pl.when(present(c))
                def _():
                    forward(c, p)

    for p in range(parts):
        relay(0, p)
    irrep_copy.wait()
    mine = wanted(col)
    for p in range(parts):
        spread(0, p)
    third = jnp.int32(0)
    for column in range(cols):
        for plane in range(bulk):
            low = irrep_ref[(2 * column * bulk + plane) * tiles]
            high = irrep_ref[((2 * column + 1) * bulk + plane) * tiles + tiles - 1]
            third = third + (high > low + 1).astype(jnp.int32)
    flag_ref[0] = third
    int_copy.wait()
    for k in range(bulk):
        for t in range(tiles):
            lhs[k, t] = ints[t, :, k * depth:(k + 1) * depth]
    res_copy.wait()
    for d in range(1, bulk):
        for p in range(parts):
            for c in groups[d]:
                @pl.when(present(c))
                def _():
                    line_in(c, p).wait_recv()
                    if d < bulk - 1:
                        relay(c, p)
                    spread(c, p)
        if d >= 2:
            add(d - 2)
        gather(d - 1)
    add(bulk - 2)
    gather(bulk - 1)
    for c in range(1, chunks):
        if 2 * abs(offsets[c]) >= bulk:
            @pl.when(at + offsets[c] == last)
            def _():
                product(c, 0, False, True)
                arrived(c)
                product(c, 1, False, True)

    for group in groups:
        for c in group:
            @pl.when(present(c))
            def _():
                for p in range(parts):
                    for j in range(cols):
                        over(c, p, j).wait_send()
                    for j in range(1, cols):
                        across(c, p, j).wait_send()
                    relay_done(c, p)


def call(rows, bulk, slots, integrals, amplitudes, residual_in, tile_irrep):
    irreps, depth, width = amplitudes.shape
    parts = PARTS if depth % (16 * PARTS) == 0 else 1
    chunks = 2 * bulk - 1
    cols = rows // 2
    any_space = pl.BlockSpec(memory_space=pltpu.HBM)
    return pl.pallas_call(
        functools.partial(kernel, rows, bulk, slots, parts),
        out_shape=(
            jax.ShapeDtypeStruct(residual_in.shape, residual_in.dtype),
            jax.ShapeDtypeStruct((1,), jnp.int32),
        ),
        in_specs=[any_space] * 4,
        out_specs=(pl.BlockSpec(memory_space=pltpu.VMEM), pl.BlockSpec(memory_space=pltpu.SMEM)),
        scratch_shapes=[
            pltpu.SMEM(tile_irrep.shape, tile_irrep.dtype),
            pltpu.VMEM(amplitudes.shape, amplitudes.dtype),
            pltpu.VMEM(integrals.shape, integrals.dtype),
            pltpu.VMEM(residual_in.shape, residual_in.dtype),
            pltpu.VMEM((bulk, *integrals.shape[:2], depth), integrals.dtype),
            pltpu.VMEM((2, *residual_in.shape[:2], cols * width), jnp.float32),
            *[pltpu.VMEM((slots, depth, cols * width), amplitudes.dtype)] * (2 * chunks),
            *[pltpu.VMEM((irreps, depth // parts, width), amplitudes.dtype)] * ((chunks - 1) * parts),
            *[pltpu.VMEM((cols - 1, slots, depth // parts, width), amplitudes.dtype)] * (chunks * parts),
            pltpu.SemaphoreType.DMA((2, chunks, parts)),
            pltpu.SemaphoreType.DMA((chunks, parts)),
            pltpu.SemaphoreType.DMA((chunks, parts, cols)),
            pltpu.SemaphoreType.DMA((chunks, parts, cols)),
            pltpu.SemaphoreType.DMA((chunks, parts, cols)),
            pltpu.SemaphoreType.DMA((chunks, parts, cols)),
            pltpu.SemaphoreType.DMA((4,)),
        ],
        compiler_params=pltpu.CompilerParams(collective_id=slots, has_side_effects=True, vmem_limit_bytes=VMEM_LIMIT),
    )(tile_irrep, amplitudes, integrals, residual_in)


def local(rows, bulk, integrals, amplitudes, residual_in, tile_irrep):
    depth, width = amplitudes.shape[1:]
    if rows % 2 or rows < 4 or bulk < 2 or depth % 16 or width % 128:
        return gathered_plan(integrals, amplitudes, residual_in, tile_irrep)
    out, third = call(rows, bulk, 2, integrals, amplitudes, residual_in, tile_irrep)
    return lax.cond(
        third[0] > 0,
        lambda out, *args: call(rows, bulk, 3, *args)[0],
        lambda out, *args: out,
        out, integrals, amplitudes, residual_in, tile_irrep)


def solution(mesh):
    return jax.shard_map(
        functools.partial(local, mesh.shape["tile"], mesh.shape["bulk"]),
        mesh=mesh,
        in_specs=(
            P(("tile", "bulk"), None, None),
            P(None, "bulk", "tile"),
            P(("tile", "bulk"), None, None),
            P(),
        ),
        out_specs=P(("tile", "bulk"), None, None),
        check_vma=False,
    )
```

time: 32.6 us -> 29.4 us (0.902)
  Pallas kernels: 29.1 us -> 27.3 us
  local copies, waits for them, and re-layouts: 1.91 us -> 1.16 us
  other arithmetic: 0.73 us -> 0 us
    pallas_call x1, Pallas kernels: 29.1 us -> 27.3 us  [call(): pl.pallas_call(functools.partial(kernel, rows, bulk, slots, parts), out_s...]
    reshape x1 -> x0, local copies, waits for them, and re-layouts: 0.76 us -> none  [local(): ends = tile_irrep.reshape(rows // 2, 2, bulk, integrals.shape[0])]
    reduce_or x1 -> x0, other arithmetic: 0.73 us -> none  [local(): jnp.any((mid != low) & (mid != high) | (mid_too != low) & (mid_too != high))]
    unnamed x1 -> x9, local copies, waits for them, and re-layouts: 1.15 us -> 1.16 us
where the time goes in v1:
time: 29.4 us; the launch traced here: 29.3 us
  Pallas kernels  27.3 us (93%)
  local copies, waits for them, and re-layouts  1.16 us (4%)
  between operations  0.62 us (2%)
    pallas_call x1, Pallas kernels, call(): pl.pallas_call(functools.partial(kernel, rows, bulk, slots, parts), out_s...  27.3 us
    unnamed x9, local copies, waits for them, and re-layouts  1.16 us

profile of v1, /device:TPU:1, one launch (start us, length us, event | category | flops | bytes accessed | tf_op | source)
XLA Modules:
  0.0 29.3 jit_solution(17911480537641054552)
XLA Ops:
  0.0 0.0 copy-start.3
  0.0 0.0 copy-start
  0.0 0.0 copy-start.2
  0.0 0.0 copy-start.1
  0.0 27.3 %shard_map.48 = (bf16[3,256,1024]{2,1,0:T(8,128)(2,1)S(1)}, s32[1]{0:T(128)}) custom-call(s32[96]{0:T(128)} %irrep_hbm.1, bf16[4,192,128]{2,1,0:T(8,128)(2,1)} %amp_hbm.1, bf16[3,256,768]{2,1,0:T(8,128)(2,1)} %int_hbm.1, bf16[3,256,1024]{2,1,0:T(8,128)(2,1)} %res_hbm.1), custom_call_target="tpu_custom_call" | custom-call | tf_op jit(solution)/shard_map/pallas_call | solution.py:257
  27.8 0.0 copy-done.3
  27.8 0.0 copy-done
  27.9 0.0 copy-done.2
  27.9 0.0 copy-done.1
  27.9 0.2 conditional.1
  28.1 1.1 %copy.10 = bf16[3,256,1024]{2,1,0:T(8,128)(2,1)} copy(bf16[3,256,1024]{2,1,0:T(8,128)(2,1)S(1)} %get-tuple-element.26) | data formatting | bytes 3145728
Async XLA Ops:
  0.0 27.8 %copy-start.3 = (s32[96]{0:T(128)S(1)}, s32[96]{0:T(128)}, u32[]{:S(2)}) copy-start(s32[96]{0:T(128)} %irrep_hbm.1) | copy-start | bytes 1156
  0.0 27.8 %copy-start = (bf16[3,256,1024]{2,1,0:T(8,128)(2,1)S(1)}, bf16[3,256,1024]{2,1,0:T(8,128)(2,1)}, u32[]{:S(2)}) copy-start(bf16[3,256,1024]{2,1,0:T(8,128)(2,1)} %res_hbm.1) | copy-start | bytes 4718596
  0.0 27.9 %copy-start.2 = (bf16[4,192,128]{2,1,0:T(8,128)(2,1)S(1)}, bf16[4,192,128]{2,1,0:T(8,128)(2,1)}, u32[]{:S(2)}) copy-start(bf16[4,192,128]{2,1,0:T(8,128)(2,1)} %amp_hbm.1) | copy-start | bytes 589828
  0.0 27.9 %copy-start.1 = (bf16[3,256,768]{2,1,0:T(8,128)(2,1)S(1)}, bf16[3,256,768]{2,1,0:T(8,128)(2,1)}, u32[]{:S(2)}) copy-start(bf16[3,256,768]{2,1,0:T(8,128)(2,1)} %int_hbm.1) | copy-start | bytes 3538948

commit v2 on v1

v2 whole, which is shorter than its diff:
```python
import functools

import jax
import jax.numpy as jnp
from jax import lax
from jax.experimental import pallas as pl
from jax.experimental.pallas import tpu as pltpu
from jax.sharding import PartitionSpec as P

MESH = pl.DeviceIdType.MESH
def gathered_plan(integrals, amplitudes, residual_in, tile_irrep):
    tile_dev = integrals.shape[0]
    first_tile = (lax.axis_index("tile") * lax.axis_size("bulk") + lax.axis_index("bulk")) * tile_dev
    local_irrep = lax.dynamic_slice_in_dim(tile_irrep, first_tile, tile_dev, 0)
    whole_cd = lax.all_gather(amplitudes, "bulk", axis=1, tiled=True)
    picked = jnp.take(lax.all_gather(whole_cd, "tile", axis=2, tiled=True), local_irrep, axis=0)
    product = jnp.einsum("trc,tcp->trp", integrals, picked, preferred_element_type=jnp.float32)
    return (residual_in.astype(jnp.float32) + product).astype(jnp.bfloat16)


VMEM_LIMIT = 32 << 20
PLANES = 4


def kernel(rows, slots, parts, irrep_hbm, amp_hbm, int_hbm, res_hbm, out_ref, flag_hbm, *scratch):
    cols = rows // 2
    bulk = PLANES
    irrep_ref, flag, amp, ints, res, lhs, total = scratch[:7]
    scratch = scratch[7:]
    gathered, scratch = [scratch[:bulk], scratch[bulk:2 * bulk]], scratch[2 * bulk:]
    units = [1] + [parts] * (bulk - 1)
    held, picked = [None], []
    for q in range(1, bulk):
        held.append(scratch[:parts])
        scratch = scratch[parts:]
    for q in range(bulk):
        picked.append(scratch[:units[q]])
        scratch = scratch[units[q]:]
    z_send, z_recv, c_send, c_recv, p_send, p_recv, local_sem = scratch
    tiles = ints.shape[0]
    depth, width = amp.shape[1:]
    piece = depth // parts
    me, at = lax.axis_index("tile"), lax.axis_index("bulk")
    col, core = me // 2, me % 2
    partner = col * 2 + (1 - core)
    lower = at < bulk // 2
    inner = jnp.logical_and(at > 0, at < bulk - 1)
    end = jnp.where(lower, 0, bulk - 1)
    beside = jnp.where(inner, end, jnp.where(lower, 1, bulk - 2))
    across_middle = bulk - 1 - at

    first, second = inner.astype(jnp.int32), 1 - inner.astype(jnp.int32)
    plane = [jnp.where(lower, p, bulk - 1 - p) for p in (first, second, 2, 3)]

    irrep_copy = pltpu.make_async_copy(irrep_hbm, irrep_ref, local_sem.at[0])
    amp_copy = pltpu.make_async_copy(amp_hbm, amp, local_sem.at[1])
    int_copy = pltpu.make_async_copy(int_hbm, ints, local_sem.at[2])
    res_copy = pltpu.make_async_copy(res_hbm, res, local_sem.at[3])
    flag_copy = pltpu.make_async_copy(flag, flag_hbm, local_sem.at[4])
    amp_copy.start()
    irrep_copy.start()

    barrier = pltpu.get_barrier_semaphore()
    pl.semaphore_signal(barrier, inc=1, device_id=(partner, at), device_id_type=MESH)
    pl.semaphore_signal(barrier, inc=1, device_id=(me, beside), device_id_type=MESH)
    for j in range(1, cols):
        pl.semaphore_signal(barrier, inc=1, device_id=(lax.rem(col + j, cols) * 2 + core, at), device_id_type=MESH)

    @pl.when(inner)
    def _():
        pl.semaphore_signal(barrier, inc=1, device_id=(me, across_middle), device_id_type=MESH)

    int_copy.start()
    res_copy.start()
    pl.semaphore_wait(barrier, cols + 1 + first)
    amp_copy.wait()

    def band(p):
        return pl.ds(p * piece, piece)

    def line(way, p):
        src_q, dst_q = ((0, 1), (0, 2), (1, 3), (2, 2), (3, 3))[way]
        there = across_middle if way in (1, 2) else beside
        return pltpu.make_async_remote_copy(
            src_ref=amp.at[:, band(p), :] if src_q == 0 else held[src_q][p], dst_ref=held[dst_q][p],
            send_sem=z_send.at[way, p], recv_sem=z_recv.at[dst_q, p], device_id=(me, there), device_id_type=MESH)

    def line_in(q, p):
        pltpu.make_async_remote_copy(
            src_ref=held[q][p], dst_ref=held[q][p], send_sem=z_send.at[0, p],
            recv_sem=z_recv.at[q, p], device_id=(partner, at), device_id_type=MESH).wait_recv()

    def relay(q, p):
        @pl.when(inner)
        def _():
            line(q + 1, p).start()

    def rows_of(q, u):
        return pl.ds(0, depth) if units[q] == 1 else band(u)

    def slab(side, q, u, column):
        return gathered[side][q].at[:, rows_of(q, u), pl.ds(pl.multiple_of(column * width, 128), width)]

    def across(q, u, j):
        return pltpu.make_async_remote_copy(
            src_ref=picked[q][u].at[j - 1], dst_ref=slab(0, q, u, col), send_sem=c_send.at[q, u, j],
            recv_sem=c_recv.at[q, u, j], device_id=(lax.rem(col + j, cols) * 2 + core, at), device_id_type=MESH)

    def over(q, u, j):
        column = lax.rem(col - j + cols, cols)
        return pltpu.make_async_remote_copy(
            src_ref=slab(0, q, u, column), dst_ref=slab(1, q, u, column), send_sem=p_send.at[q, u, j],
            recv_sem=p_recv.at[q, u, j], device_id=(partner, at), device_id_type=MESH)

    def wanted(column):
        low = (2 * column * bulk + at) * tiles
        high = ((2 * column + 1) * bulk + at) * tiles + tiles - 1
        spots = [low, high] if slots == 2 else [low, low + tiles - 1, high]
        return [irrep_ref[s] for s in spots]

    def spread(q, u):
        src = amp if q == 0 else held[q][u]
        for k in range(1, cols):
            j = lax.rem(k - 1 + (k > col).astype(jnp.int32) - col + cols, cols)
            for s, g in enumerate(wanted(lax.rem(col + j, cols))):
                picked[q][u][j - 1, s] = src[g]
            across(q, u, j).start()
        for s, g in enumerate(mine):
            gathered[0][q][s, rows_of(q, u), pl.ds(pl.multiple_of(col * width, 128), width)] = src[g]
        over(q, u, 0).start()

    def forward(q):
        for u in range(units[q]):
            for j in range(1, cols):
                landed = slab(0, q, u, lax.rem(col - j + cols, cols))
                pltpu.make_async_remote_copy(
                    src_ref=landed, dst_ref=landed, send_sem=c_send.at[q, u, j], recv_sem=c_recv.at[q, u, j],
                    device_id=(partner, at), device_id_type=MESH).wait_recv()
                over(q, u, j).start()

    first_tile = (me * bulk + at) * tiles

    def product(q, side):
        for t in range(tiles):
            irrep = irrep_ref[first_tile + t]
            slot = (irrep > mine[0]).astype(jnp.int32)
            for s in mine[1:-1]:
                slot = slot + (irrep > s).astype(jnp.int32)
            part = jnp.dot(lhs[plane[q], t], gathered[side][q][slot], preferred_element_type=jnp.float32)
            if q > 0:
                part = part + total[side, t]
            if 0 < q < bulk - 1:
                total[side, t] = part
                continue
            for n in range(cols):
                there = pl.ds(pl.multiple_of((n * 2 + (core if side == 0 else 1 - core)) * width, width), width)
                here = part[:, n * width:(n + 1) * width]
                if q > 0:
                    out_ref[t, :, there] = here.astype(jnp.bfloat16)
                else:
                    total[side, t, :, n * width:(n + 1) * width] = here + res[t, :, there].astype(jnp.float32)

    def arrived(q):
        for u in range(units[q]):
            for j in range(cols):
                over(q, u, j).wait_recv()

    def add(q):
        arrived(q)
        for side in range(2):
            product(q, side)

    for p in range(parts):
        line(0, p).start()

        @pl.when(inner)
        def _():
            line(1, p).start()

    irrep_copy.wait()
    mine = wanted(col)
    spread(0, 0)
    third = jnp.int32(0)
    for column in range(cols):
        for level in range(bulk):
            low = irrep_ref[(2 * column * bulk + level) * tiles]
            high = irrep_ref[((2 * column + 1) * bulk + level) * tiles + tiles - 1]
            third = third + (high > low + 1).astype(jnp.int32)
    flag[0] = third
    flag_copy.start()
    int_copy.wait()
    for k in range(bulk):
        for t in range(tiles):
            lhs[k, t] = ints[t, :, k * depth:(k + 1) * depth]
    res_copy.wait()
    flag_copy.wait()

    for p in range(parts):
        line_in(1, p)
        relay(1, p)
        spread(1, p)
        if p < parts - 1:
            @pl.when(inner)
            def _():
                line_in(2, p)
                line(3, p).start()
    for p in range(parts):
        if p < parts - 1:
            @pl.when(jnp.logical_not(inner))
            def _():
                line_in(2, p)
        else:
            line_in(2, p)
            relay(2, p)
        spread(2, p)
    forward(0)
    for p in range(parts):
        line_in(3, p)
        relay(3, p)
        spread(3, p)
    add(0)
    forward(1)
    add(1)
    forward(2)
    add(2)
    forward(3)
    product(3, 0)
    arrived(3)
    product(3, 1)

    for q in range(bulk):
        for u in range(units[q]):
            for j in range(cols):
                over(q, u, j).wait_send()
            for j in range(1, cols):
                across(q, u, j).wait_send()
    for p in range(parts):
        line(0, p).wait_send()

        @pl.when(inner)
        def _():
            for way in range(1, 5):
                line(way, p).wait_send()


def call(rows, slots, integrals, amplitudes, residual_in, tile_irrep):
    irreps, depth, width = amplitudes.shape
    tiles, height = integrals.shape[:2]
    parts = 2 if depth % 32 == 0 else 1
    bulk = PLANES
    cols = rows // 2
    hbm = pl.BlockSpec(memory_space=pltpu.HBM)
    kind = amplitudes.dtype
    picked = [depth] + [depth // parts] * (parts * (bulk - 1))
    return pl.pallas_call(
        functools.partial(kernel, rows, slots, parts),
        out_shape=(
            jax.ShapeDtypeStruct(residual_in.shape, residual_in.dtype),
            jax.ShapeDtypeStruct((1,), jnp.int32),
        ),
        in_specs=[hbm] * 4,
        out_specs=(pl.BlockSpec(memory_space=pltpu.VMEM), hbm),
        scratch_shapes=[
            pltpu.SMEM(tile_irrep.shape, tile_irrep.dtype),
            pltpu.SMEM((1,), jnp.int32),
            pltpu.VMEM(amplitudes.shape, kind),
            pltpu.VMEM(integrals.shape, integrals.dtype),
            pltpu.VMEM(residual_in.shape, residual_in.dtype),
            pltpu.VMEM((bulk, tiles, height, depth), integrals.dtype),
            pltpu.VMEM((2, tiles, height, cols * width), jnp.float32),
            *[pltpu.VMEM((slots, depth, cols * width), kind)] * (2 * bulk),
            *[pltpu.VMEM((irreps, depth // parts, width), kind)] * (parts * (bulk - 1)),
            *[pltpu.VMEM((cols - 1, slots, size, width), kind) for size in picked],
            pltpu.SemaphoreType.DMA((5, parts)),
            pltpu.SemaphoreType.DMA((bulk, parts)),
            *[pltpu.SemaphoreType.DMA((bulk, parts, cols))] * 4,
            pltpu.SemaphoreType.DMA((5,)),
        ],
        compiler_params=pltpu.CompilerParams(collective_id=slots, has_side_effects=True, vmem_limit_bytes=VMEM_LIMIT),
    )(tile_irrep, amplitudes, integrals, residual_in)


def local(rows, bulk, integrals, amplitudes, residual_in, tile_irrep):
    depth, width = amplitudes.shape[1:]
    if rows % 2 or rows < 4 or bulk != PLANES or depth % 16 or width % 128:
        return gathered_plan(integrals, amplitudes, residual_in, tile_irrep)
    out, third = call(rows, 2, integrals, amplitudes, residual_in, tile_irrep)
    return lax.cond(
        third[0] > 0,
        lambda out, *args: call(rows, 3, *[pltpu.with_memory_space_constraint(x, pltpu.HBM) for x in args])[0],
        lambda out, *args: out,
        out, integrals, amplitudes, residual_in, tile_irrep)


def solution(mesh):
    return jax.shard_map(
        functools.partial(local, mesh.shape["tile"], mesh.shape["bulk"]),
        mesh=mesh,
        in_specs=(
            P(("tile", "bulk"), None, None),
            P(None, "bulk", "tile"),
            P(("tile", "bulk"), None, None),
            P(),
        ),
        out_specs=P(("tile", "bulk"), None, None),
        check_vma=False,
    )
```

time: 29.4 us -> 28.3 us (0.963)
  Pallas kernels: 27.3 us -> 26.3 us
    pallas_call x1, Pallas kernels: 27.3 us -> 26.3 us  [call(): pl.pallas_call(functools.partial(kernel, rows, slots, parts), out_shape=(...]
    unnamed x9 -> x1, local copies, waits for them, and re-layouts: 1.16 us -> 1.15 us
where the time goes in v2:
time: 28.3 us; the launch traced here: 28.1 us
  Pallas kernels  26.3 us (93%)
  local copies, waits for them, and re-layouts  1.15 us (4%)
  between operations  0.63 us (2%)
    pallas_call x1, Pallas kernels, call(): pl.pallas_call(functools.partial(kernel, rows, slots, parts), out_shape=(...  26.3 us
    unnamed x1, local copies, waits for them, and re-layouts  1.15 us

profile of v2, /device:TPU:1, one launch (start us, length us, event | category | flops | bytes accessed | tf_op | source)
XLA Modules:
  0.0 28.1 jit_solution(10794389655320271249)
XLA Ops:
  0.0 26.3 %shard_map.48 = (bf16[3,256,1024]{2,1,0:T(8,128)(2,1)S(1)}, s32[1]{0:T(128)}) custom-call(s32[96]{0:T(128)} %irrep_hbm.1, bf16[4,192,128]{2,1,0:T(8,128)(2,1)} %amp_hbm.1, bf16[3,256,768]{2,1,0:T(8,128)(2,1)} %int_hbm.1, bf16[3,256,1024]{2,1,0:T(8,128)(2,1)} %res_hbm.1), custom_call_target="tpu_custom_call" | custom-call | tf_op jit(solution)/shard_map/pallas_call | solution.py:255
  27.0 1.1 %copy.10 = bf16[3,256,1024]{2,1,0:T(8,128)(2,1)} copy(bf16[3,256,1024]{2,1,0:T(8,128)(2,1)S(1)} %get-tuple-element.26) | data formatting | bytes 3145728
  (1 shorter events, 0.0 us)

commit v3 on v2

--- a/solution.py
+++ b/solution.py
@@ -90,11 +90,6 @@
             src_ref=held[q][p], dst_ref=held[q][p], send_sem=z_send.at[0, p],
             recv_sem=z_recv.at[q, p], device_id=(partner, at), device_id_type=MESH).wait_recv()
 
-    def relay(q, p):
-        @pl.when(inner)
-        def _():
-            line(q + 1, p).start()
-
     def rows_of(q, u):
         return pl.ds(0, depth) if units[q] == 1 else band(u)
 
@@ -197,31 +192,37 @@
 
     for p in range(parts):
         line_in(1, p)
-        relay(1, p)
+
+        @pl.when(inner)
+        def _():
+            line(2, p).start()
+            line_in(2, p)
+            line(3, p).start()
+
         spread(1, p)
-        if p < parts - 1:
-            @pl.when(inner)
-            def _():
-                line_in(2, p)
-                line(3, p).start()
-    for p in range(parts):
-        if p < parts - 1:
-            @pl.when(jnp.logical_not(inner))
-            def _():
-                line_in(2, p)
-        else:
+    for p in range(parts):
+        @pl.when(jnp.logical_not(inner))
+        def _():
             line_in(2, p)
-            relay(2, p)
+
         spread(2, p)
+    @pl.when(inner)
+    def _():
+        for p in range(parts):
+            line_in(3, p)
+            line(4, p).start()
+
     forward(0)
     for p in range(parts):
-        line_in(3, p)
-        relay(3, p)
+        @pl.when(jnp.logical_not(inner))
+        def _():
+            line_in(3, p)
+
         spread(3, p)
+    forward(1)
     add(0)
-    forward(1)
+    forward(2)
     add(1)
-    forward(2)
     add(2)
     forward(3)
     product(3, 0)

time: 28.3 us -> 27.4 us (0.968)
  Pallas kernels: 26.3 us -> 25.5 us
    pallas_call x1, Pallas kernels: 26.3 us -> 25.5 us  [call(): pl.pallas_call(functools.partial(kernel, rows, slots, parts), out_shape=(...]
where the time goes in v3:
time: 27.4 us; the launch traced here: 27.2 us
  Pallas kernels  25.5 us (93%)
  local copies, waits for them, and re-layouts  1.15 us (4%)
  between operations  0.63 us (2%)
    pallas_call x1, Pallas kernels, call(): pl.pallas_call(functools.partial(kernel, rows, slots, parts), out_shape=(...  25.5 us
    unnamed x1, local copies, waits for them, and re-layouts  1.15 us

profile of v3, /device:TPU:1, one launch (start us, length us, event | category | flops | bytes accessed | tf_op | source)
XLA Modules:
  0.0 27.2 jit_solution(10267583576698917297)
XLA Ops:
  0.0 25.5 %shard_map.48 = (bf16[3,256,1024]{2,1,0:T(8,128)(2,1)S(1)}, s32[1]{0:T(128)}) custom-call(s32[96]{0:T(128)} %irrep_hbm.1, bf16[4,192,128]{2,1,0:T(8,128)(2,1)} %amp_hbm.1, bf16[3,256,768]{2,1,0:T(8,128)(2,1)} %int_hbm.1, bf16[3,256,1024]{2,1,0:T(8,128)(2,1)} %res_hbm.1), custom_call_target="tpu_custom_call" | custom-call | tf_op jit(solution)/shard_map/pallas_call | solution.py:256
  26.1 1.1 %copy.10 = bf16[3,256,1024]{2,1,0:T(8,128)(2,1)} copy(bf16[3,256,1024]{2,1,0:T(8,128)(2,1)S(1)} %get-tuple-element.26) | data formatting | bytes 3145728
  (1 shorter events, 0.0 us)

commit v4 on v3

--- a/solution.py
+++ b/solution.py
@@ -20,6 +20,7 @@
 
 VMEM_LIMIT = 32 << 20
 PLANES = 4
+COLUMNS = 4
 
 
 def kernel(rows, slots, parts, irrep_hbm, amp_hbm, int_hbm, res_hbm, out_ref, flag_hbm, *scratch):
@@ -36,7 +37,7 @@
     for q in range(bulk):
         picked.append(scratch[:units[q]])
         scratch = scratch[units[q]:]
-    z_send, z_recv, c_send, c_recv, p_send, p_recv, local_sem = scratch
+    z_send, z_recv, c_send, c_recv, p_send, p_recv, local_sem, vouched = scratch
     tiles = ints.shape[0]
     depth, width = amp.shape[1:]
     piece = depth // parts
@@ -60,11 +61,15 @@
     amp_copy.start()
     irrep_copy.start()
 
+    odd, half = col % 2, col // 2
+    near = [half * 2 + 1 - odd, (1 - half) * 2 + odd]
+    far = (1 - half) * 2 + 1 - odd
+
     barrier = pltpu.get_barrier_semaphore()
     pl.semaphore_signal(barrier, inc=1, device_id=(partner, at), device_id_type=MESH)
     pl.semaphore_signal(barrier, inc=1, device_id=(me, beside), device_id_type=MESH)
-    for j in range(1, cols):
-        pl.semaphore_signal(barrier, inc=1, device_id=(lax.rem(col + j, cols) * 2 + core, at), device_id_type=MESH)
+    for column in near:
+        pl.semaphore_signal(barrier, inc=1, device_id=(column * 2 + core, at), device_id_type=MESH)
 
     @pl.when(inner)
     def _():
@@ -72,7 +77,8 @@
 
     int_copy.start()
     res_copy.start()
-    pl.semaphore_wait(barrier, cols + 1 + first)
+    pl.semaphore_wait(barrier, 2 + len(near) + first)
+    pl.semaphore_signal(vouched, inc=1, device_id=(near[0] * 2 + core, at), device_id_type=MESH)
     amp_copy.wait()
 
     def band(p):
@@ -115,10 +121,13 @@
 
     def spread(q, u):
         src = amp if q == 0 else held[q][u]
-        for k in range(1, cols):
-            j = lax.rem(k - 1 + (k > col).astype(jnp.int32) - col + cols, cols)
+        rising = [k + (k >= col).astype(jnp.int32) for k in range(cols - 1)]
+        for column in (near[1], near[0], far) if q == 0 else rising:
+            j = lax.rem(column - col + cols, cols)
             for s, g in enumerate(wanted(lax.rem(col + j, cols))):
                 picked[q][u][j - 1, s] = src[g]
+            if q == 0 and column is far:
+                pl.semaphore_wait(vouched, 1)
             across(q, u, j).start()
         for s, g in enumerate(mine):
             gathered[0][q][s, rows_of(q, u), pl.ds(pl.multiple_of(col * width, 128), width)] = src[g]
@@ -126,8 +135,9 @@
 
     def forward(q):
         for u in range(units[q]):
-            for j in range(1, cols):
-                landed = slab(0, q, u, lax.rem(col - j + cols, cols))
+            for column in (*near, far):
+                j = lax.rem(col - column + cols, cols)
+                landed = slab(0, q, u, column)
                 pltpu.make_async_remote_copy(
                     src_ref=landed, dst_ref=landed, send_sem=c_send.at[q, u, j], recv_sem=c_recv.at[q, u, j],
                     device_id=(partner, at), device_id_type=MESH).wait_recv()
@@ -276,6 +286,7 @@
             pltpu.SemaphoreType.DMA((bulk, parts)),
             *[pltpu.SemaphoreType.DMA((bulk, parts, cols))] * 4,
             pltpu.SemaphoreType.DMA((5,)),
+            pltpu.SemaphoreType.REGULAR,
         ],
         compiler_params=pltpu.CompilerParams(collective_id=slots, has_side_effects=True, vmem_limit_bytes=VMEM_LIMIT),
     )(tile_irrep, amplitudes, integrals, residual_in)
@@ -283,7 +294,7 @@
 
 def local(rows, bulk, integrals, amplitudes, residual_in, tile_irrep):
     depth, width = amplitudes.shape[1:]
-    if rows % 2 or rows < 4 or bulk != PLANES or depth % 16 or width % 128:
+    if rows != 2 * COLUMNS or bulk != PLANES or depth % 16 or width % 128:
         return gathered_plan(integrals, amplitudes, residual_in, tile_irrep)
     out, third = call(rows, 2, integrals, amplitudes, residual_in, tile_irrep)
     return lax.cond(

time: 27.4 us -> 27.2 us (level)
  no operation moved by 1% of the time
where the time goes in v4:
time: 27.2 us; the launch traced here: 27 us
  Pallas kernels  25.3 us (93%)
  local copies, waits for them, and re-layouts  1.15 us (4%)
  between operations  0.63 us (2%)
    pallas_call x1, Pallas kernels, call(): pl.pallas_call(functools.partial(kernel, rows, slots, parts), out_shape=(...  25.3 us
    unnamed x1, local copies, waits for them, and re-layouts  1.15 us

profile of v4, /device:TPU:1, one launch (start us, length us, event | category | flops | bytes accessed | tf_op | source)
XLA Modules:
  0.0 27.0 jit_solution(10715550614794906397)
XLA Ops:
  0.0 25.3 %shard_map.48 = (bf16[3,256,1024]{2,1,0:T(8,128)(2,1)S(1)}, s32[1]{0:T(128)}) custom-call(s32[96]{0:T(128)} %irrep_hbm.1, bf16[4,192,128]{2,1,0:T(8,128)(2,1)} %amp_hbm.1, bf16[3,256,768]{2,1,0:T(8,128)(2,1)} %int_hbm.1, bf16[3,256,1024]{2,1,0:T(8,128)(2,1)} %res_hbm.1), custom_call_target="tpu_custom_call" | custom-call | tf_op jit(solution)/shard_map/pallas_call | solution.py:266
  25.9 1.1 %copy.10 = bf16[3,256,1024]{2,1,0:T(8,128)(2,1)} copy(bf16[3,256,1024]{2,1,0:T(8,128)(2,1)S(1)} %get-tuple-element.26) | data formatting | bytes 3145728
  (1 shorter events, 0.0 us)

commit v5 on v4

--- a/solution.py
+++ b/solution.py
@@ -133,8 +133,8 @@
             gathered[0][q][s, rows_of(q, u), pl.ds(pl.multiple_of(col * width, 128), width)] = src[g]
         over(q, u, 0).start()
 
-    def forward(q):
-        for u in range(units[q]):
+    def forward(q, only=None):
+        for u in range(units[q]) if only is None else only:
             for column in (*near, far):
                 j = lax.rem(col - column + cols, cols)
                 landed = slab(0, q, u, column)
@@ -233,18 +233,18 @@
     add(0)
     forward(2)
     add(1)
+    forward(3, range(units[3] - 1))
     add(2)
-    forward(3)
+    forward(3, [units[3] - 1])
     product(3, 0)
-    arrived(3)
-    product(3, 1)
 
     for q in range(bulk):
         for u in range(units[q]):
             for j in range(cols):
-                over(q, u, j).wait_send()
-            for j in range(1, cols):
-                across(q, u, j).wait_send()
+                if q < bulk - 1:
+                    over(q, u, j).wait_send()
+                if j > 0:
+                    across(q, u, j).wait_send()
     for p in range(parts):
         line(0, p).wait_send()
 
@@ -252,6 +252,12 @@
         def _():
             for way in range(1, 5):
                 line(way, p).wait_send()
+
+    arrived(3)
+    product(3, 1)
+    for u in range(units[3]):
+        for j in range(cols):
+            over(3, u, j).wait_send()
 
 
 def call(rows, slots, integrals, amplitudes, residual_in, tile_irrep):

time: 27.2 us -> 27.1 us (level)
  no operation moved by 1% of the time
where the time goes in v5:
time: 27.1 us; the launch traced here: 27 us
  Pallas kernels  25.2 us (93%)
  local copies, waits for them, and re-layouts  1.15 us (4%)
  between operations  0.63 us (2%)
    pallas_call x1, Pallas kernels, call(): pl.pallas_call(functools.partial(kernel, rows, slots, parts), out_shape=(...  25.2 us
    unnamed x1, local copies, waits for them, and re-layouts  1.15 us

profile of v5, /device:TPU:1, one launch (start us, length us, event | category | flops | bytes accessed | tf_op | source)
XLA Modules:
  0.0 27.0 jit_solution(9096748993976045324)
XLA Ops:
  0.0 25.2 %shard_map.48 = (bf16[3,256,1024]{2,1,0:T(8,128)(2,1)S(1)}, s32[1]{0:T(128)}) custom-call(s32[96]{0:T(128)} %irrep_hbm.1, bf16[4,192,128]{2,1,0:T(8,128)(2,1)} %amp_hbm.1, bf16[3,256,768]{2,1,0:T(8,128)(2,1)} %int_hbm.1, bf16[3,256,1024]{2,1,0:T(8,128)(2,1)} %res_hbm.1), custom_call_target="tpu_custom_call" | custom-call | tf_op jit(solution)/shard_map/pallas_call | solution.py:272
  25.8 1.1 %copy.10 = bf16[3,256,1024]{2,1,0:T(8,128)(2,1)} copy(bf16[3,256,1024]{2,1,0:T(8,128)(2,1)S(1)} %get-tuple-element.26) | data formatting | bytes 3145728
  (1 shorter events, 0.0 us)
